TPU v7x, 32 devices: a whole 2x2x4 slice. The times are simulated.
32 devices in a mesh: gx: 4 (over x, core), yz: 8 (over z, y).
Axes of the slice: x: 2, y: 2, z: 4, core: 2. Of those that a mesh axis runs over, the one named last changes fastest.
Arguments:
- fine_blocks: bfloat16 [256, 1536, 512], P(('gx', 'yz')), may hold values from -6 to 6
- fine_to_coarse: int32 [256], replicated, may hold values from 0 to 127, as said below
- widths: int32 [256], P(('gx', 'yz')), may hold values from 256 to 512
- pivots: int32 [128, 1024], P(('gx', 'yz')), may hold values from 0 to 1023, as said below
- neighbours: int32 [128, 4], P(('gx', 'yz')), may hold values from 0 to 3
Outputs:
- interp: float32 [128, 384, 640], P(('gx', 'yz'))
- schur_blocks: float32 [128, 384, 384], P(('gx', 'yz'))
Inputs may be any that keep to these rules, and one draw needn't show every extreme that they name: `fine_to_coarse`: cluster c is owned by the device of index c // 4 along gx+yz, which has the same gx index as both its fine blocks; each cluster has exactly two fine blocks, on different devices, and the 8 blocks of one device belong to clusters of 8 different devices. `pivots`: each row is a permutation of 0 to 1023 whose first 384 entries are live columns (below the width of the first block, or 512 plus a column below the width of the second).
All inputs are finite; a program needn't handle non-finite values.
Results may differ from a plain program's by a relative error of at most 0.0003.
Values may be sent and summed in bfloat16 or wider, within the bound.
A program may use at most 192 MiB of HBM per device.

v0:
```python
import jax
import jax.numpy as jnp
from jax import lax
from jax.sharding import PartitionSpec as P

K = 384


def with_halo(cells, sides, width):
    for axis, dim in sides:
        count = lax.axis_size(axis)
        ends = count - 1
        head = lax.slice_in_dim(cells, 0, width, axis=dim)
        tail = lax.slice_in_dim(cells, cells.shape[dim] - width, cells.shape[dim], axis=dim)
        cells = jnp.concatenate(
            [
                lax.ppermute(tail, axis, [(i, (i + 1) % count) for i in range(ends)]),
                cells,
                lax.ppermute(head, axis, [((i + 1) % count, i) for i in range(ends)]),
            ],
            axis=dim,
        )
    return cells


def interpolate(gram_rows, kept_cols):
    factor = jnp.linalg.cholesky(gram_rows[:, :, :kept_cols])
    half_solved = jax.scipy.linalg.solve_triangular(factor, gram_rows[:, :, kept_cols:], lower=True)
    return jax.scipy.linalg.solve_triangular(factor, half_solved, lower=True, trans=1)


def pick_sides(nearby, neighbours):
    side_terms = jnp.stack([nearby[0, 1], nearby[2, 1], nearby[1, 0], nearby[1, 2]])
    cluster_count = side_terms.shape[1]
    flattened = side_terms.reshape((4 * cluster_count,) + side_terms.shape[2:])
    flat_index = jnp.arange(4, dtype=jnp.int32)[None, :] * cluster_count + neighbours
    chosen = jnp.take(flattened, flat_index.reshape(-1), axis=0)
    return chosen.reshape((cluster_count, 4) + side_terms.shape[2:])


def body(fine_blocks, fine_to_coarse, widths, pivots, neighbours):
    gx_count = lax.axis_size("gx")
    yz_count = lax.axis_size("yz")
    gx_pos = lax.axis_index("gx")
    yz_pos = lax.axis_index("yz")
    blocks_dev = fine_blocks.shape[0]
    col_count = fine_blocks.shape[2]
    clusters = blocks_dev // 2
    kept_cols = K
    device = gx_pos * yz_count + yz_pos
    cluster_table = fine_to_coarse.reshape(gx_count, yz_count, blocks_dev)
    grouped = lax.dynamic_index_in_dim(cluster_table, gx_pos, 0, keepdims=False)
    own_targets = lax.dynamic_index_in_dim(grouped, yz_pos, 0, keepdims=False)
    target = own_targets // clusters - gx_pos * yz_count
    column = jnp.arange(col_count, dtype=jnp.int32)
    live_cols = (column[None, :] < widths[:, None]).astype(jnp.bfloat16)
    masked = fine_blocks * live_cols[:, None, :]
    peer_ids = jnp.arange(yz_count, dtype=jnp.int32)
    matches = target[None, :] == peer_ids[:, None]
    source_slot = jnp.sum(
        jnp.where(matches, jnp.arange(blocks_dev, dtype=jnp.int32)[None, :], 0), axis=1
    )
    filled = jnp.any(matches, axis=1).astype(jnp.bfloat16)
    outgoing = jnp.take(masked, source_slot, axis=0) * filled[:, None, None]
    arrived = lax.all_to_all(outgoing, "yz", split_axis=0, concat_axis=0, tiled=True)
    owned_here = grouped // clusters == device
    local_index = jnp.sum(jnp.where(owned_here, grouped % clusters, 0), axis=1)
    arrived_any = jnp.any(owned_here, axis=1)
    member = arrived_any[None, :] & (
        local_index[None, :] == jnp.arange(clusters, dtype=jnp.int32)[:, None]
    )
    first_src = jnp.min(jnp.where(member, peer_ids[None, :], yz_count), axis=1)
    second = jnp.max(jnp.where(member, peer_ids[None, :], -1), axis=1)
    merged = jnp.concatenate(
        [jnp.take(arrived, first_src, axis=0), jnp.take(arrived, second, axis=0)], axis=2
    )
    pivoted = jnp.take_along_axis(merged, pivots[:, None, :], axis=2)
    gram_rows = jnp.einsum(
        "cpk,cpw->ckw", pivoted[:, :, :kept_cols], pivoted, preferred_element_type=jnp.float32
    )
    interp = interpolate(gram_rows, kept_cols)
    updates = jnp.einsum("ckr,cjr->ckj", interp, interp, precision=lax.Precision.HIGHEST)
    nearby = with_halo(updates[None, None], (("gx", 0), ("yz", 1)), 1)
    chosen = pick_sides(nearby, neighbours)
    schur_blocks = updates + jnp.sum(chosen, axis=1)
    return (interp, schur_blocks)


def solution(mesh):
    return jax.shard_map(
        body,
        mesh=mesh,
        in_specs=(
            P(("gx", "yz"), None, None),
            P(),
            P(("gx", "yz")),
            P(("gx", "yz"), None),
            P(("gx", "yz"), None),
        ),
        out_specs=(P(("gx", "yz"), None, None), P(("gx", "yz"), None, None)),
        check_vma=False,
    )
```

profile of v0, /device:TPU:25, one launch (start us, length us, event | category | flops | bytes accessed | tf_op | source)
XLA Modules:
  0.0 1218.9 jit_solution(12570003289146979870)
XLA Ops:
  2.4 10.7 broadcast_multiply_fusion
  13.1 10.9 gather_fusion
  24.0 10.8 select_multiply_fusion
  42.2 270.5 %all-to-all-done = bf16[8,1536,512]{2,1,0:T(8,128)(2,1)} async-done(((bf16[8,1536,512]{2,1,0:T(8,128)(2,1)}), bf16[8,1536,512]{2,1,0:T(8,128)(2,1)}, u32[]{:S(2)}, u32[]{:S(2)}) %all-to-all-start) | async-done | bytes 12582944 | tf_op jit(solution)/shard_map/all_to_all | solution.py:65
  312.7 8.1 gather_fusion.3
  320.8 6.0 broadcast_select_fusion.3
  326.9 8.1 gather_fusion.4
  339.6 5.7 pad_maximum_fusion
  345.3 16.6 %copy.26 = bf16[4,1536,1024]{1,2,0:T(8,128)(2,1)} copy(bf16[4,1536,1024]{2,1,0:T(8,128)(2,1)} %pad_maximum_fusion) | data formatting | bytes 25165824 | tf_op jit(solution)/shard_map/concatenate | solution.py:74
  361.9 91.5 %gather_fusion.2 = bf16[4096,1536]{1,0:T(8,128)(2,1)} fusion(bf16[4,1536,1024]{1,2,0:T(8,128)(2,1)} %copy.26, s32[4096]{0:T(1024)S(1)} %bitcast.114), kind=kCustom, calls=%fused_computation.4 | custom fusion | bytes 25198592 | tf_op jit(solution)/shard_map/jit(take_along_axis)/gather | solution.py:77
  453.5 10.9 fusion.1
  464.4 9.1 fusion
  483.2 46.9 %custom-call.29 = f32[4,128,128]{2,1,0:T(8,128)S(1)} custom-call(f32[4,128,128]{2,1,0:T(8,128)S(1)} %cholesky.198), custom_call_target="Cholesky" | custom-call | tf_op jit(solution)/shard_map/jit(cholesky)/cholesky | solution.py:27
  530.3 39.7 %custom-call.30 = f32[4,1,128,128]{2,3,1,0:T(8,128)S(1)} custom-call(f32[4,1,128,128]{3,2,1,0:T(8,128)S(1)} %select_bitcast_fusion.1), custom_call_target="InvertDiagBlocksLowerTriangular" | custom-call | tf_op jit(solution)/shard_map/jit(cholesky)/cholesky | solution.py:27
  574.1 47.7 %custom-call.31 = f32[4,128,128]{2,1,0:T(8,128)S(1)} custom-call(f32[4,128,128]{2,1,0:T(8,128)} %cholesky.202), custom_call_target="Cholesky" | custom-call | tf_op jit(solution)/shard_map/jit(cholesky)/cholesky | solution.py:27
  623.3 40.7 %custom-call.32 = f32[4,1,128,128]{2,3,1,0:T(8,128)} custom-call(f32[4,1,128,128]{3,2,1,0:T(8,128)} %get-tuple-element.32), custom_call_target="InvertDiagBlocksLowerTriangular" | custom-call | tf_op jit(solution)/shard_map/jit(cholesky)/cholesky | solution.py:27
  666.9 46.9 %custom-call.33 = f32[4,128,128]{2,1,0:T(8,128)S(1)} custom-call(f32[4,128,128]{2,1,0:T(8,128)S(1)} %convolution_subtract_fusion.3), custom_call_target="Cholesky" | custom-call | tf_op jit(solution)/shard_map/jit(cholesky)/cholesky | solution.py:27
  716.8 11.1 while.1
  727.9 119.0 %custom-call.34 = f32[4,3,128,128]{2,3,1,0:T(8,128)S(1)} custom-call(f32[4,3,128,128]{3,2,1,0:T(8,128)} %bitcast.123), custom_call_target="InvertDiagBlocksLowerTriangular" | custom-call | tf_op jit(solution)/shard_map/jit(_solve_triangular)/vmap()/triangular_solve | solution.py:29
  865.2 7.3 fusion.58
  878.0 23.8 %collective-permute-done = f32[1,1,4,384,384]{4,3,2,1,0:T(8,128)S(1)} collective-permute-done((f32[1,1,4,384,384]{4,3,2,1,0:T(8,128)S(1)}, f32[1,1,4,384,384]{4,3,2,1,0:T(8,128)S(1)}, u32[]{:S(2)}, u32[]{:S(2)}) %collective-permute-start) | collective-permute-done | bytes 2359328 | tf_op jit(solution)/shard_map/ppermute | solution.py:17
  912.3 6.2 collective-permute-start.2
  918.6 276.1 %collective-permute-done.3 = f32[3,1,4,384,384]{4,3,2,1,0:T(8,128)} collective-permute-done((f32[3,1,4,384,384]{4,3,2,1,0:T(8,128)}, f32[3,1,4,384,384]{4,3,2,1,0:T(8,128)}, u32[]{:S(2)}, u32[]{:S(2)}) %collective-permute-start.3) | collective-permute-done | bytes 7077920 | tf_op jit(solution)/shard_map/ppermute | solution.py:19
  1203.5 8.5 gather_fusion.1
  (107 shorter events, 95.5 us)
Async XLA Ops:
  34.8 5.6 copy-start.10
  34.8 277.9 %all-to-all-start = ((bf16[8,1536,512]{2,1,0:T(8,128)(2,1)}), bf16[8,1536,512]{2,1,0:T(8,128)(2,1)}, u32[]{:S(2)}, u32[]{:S(2)}) async-start(bf16[8,1536,512]{2,1,0:T(8,128)(2,1)} %select_multiply_fusion), calls=%async_computation | async-start | bytes 25165824 | tf_op jit(solution)/shard_map/all_to_all | solution.py:65
  41.5 488.8 %copy-start.9 = (pred[128,128]{1,0:T(8,128)(4,1)}, pred[128,128]{1,0:T(8,128)(4,1)S(1)}, u32[]{:S(2)}) copy-start(pred[128,128]{1,0:T(8,128)(4,1)S(1)} %iota_compare_fusion.1) | copy-start | bytes 49156
  335.0 4.6 copy-start.1
  473.5 2.7 copy-start.2
  481.8 1.4 copy-start.8
  715.0 1.8 copy-start.12
  727.9 121.6 %copy-start.3 = (f32[4,384,384]{2,1,0:T(8,128)S(1)}, f32[4,384,384]{2,1,0:T(8,128)}, u32[]{:S(2)}) copy-start(f32[4,384,384]{2,1,0:T(8,128)} %get-tuple-element.88) | copy-start | bytes 7077892
  865.2 7.3 copy-start
  872.6 45.9 %copy-start.11 = (s32[4,4]{1,0:T(4,128)S(1)}, s32[4,4]{1,0:T(4,128)}, u32[]{:S(2)}) copy-start(s32[4,4]{1,0:T(4,128)} %param.11) | copy-start | bytes 196
  872.6 29.3 %collective-permute-start = (f32[1,1,4,384,384]{4,3,2,1,0:T(8,128)S(1)}, f32[1,1,4,384,384]{4,3,2,1,0:T(8,128)S(1)}, u32[]{:S(2)}, u32[]{:S(2)}) collective-permute-start(f32[1,1,4,384,384]{4,3,2,1,0:T(8,128)S(1)} %bitcast.118), channel_id=1, source_target_pairs={{0,8},{8,16},{16,24},{1,9},{9,17},{17,25},{2,10},{10,18},{18,26},{... | collective-permute-start | bytes 7077896 | tf_op jit(solution)/shard_map/ppermute | solution.py:17
  876.1 30.6 %collective-permute-start.1 = (f32[1,1,4,384,384]{4,3,2,1,0:T(8,128)S(1)}, f32[1,1,4,384,384]{4,3,2,1,0:T(8,128)S(1)}, u32[]{:S(2)}, u32[]{:S(2)}) collective-permute-start(f32[1,1,4,384,384]{4,3,2,1,0:T(8,128)S(1)} %bitcast.119), channel_id=1, source_target_pairs={{8,0},{16,8},{24,16},{9,1},{17,9},{25,17},{10,2},{18,10},{26,18},{... | collective-permute-start | bytes 7077896 | tf_op jit(solution)/shard_map/ppermute | solution.py:19
  901.9 8.5 copy-start.4
  906.7 3.7 copy-start.6
  910.4 284.3 %collective-permute-start.3 = (f32[3,1,4,384,384]{4,3,2,1,0:T(8,128)}, f32[3,1,4,384,384]{4,3,2,1,0:T(8,128)}, u32[]{:S(2)}, u32[]{:S(2)}) collective-permute-start(f32[3,1,4,384,384]{4,3,2,1,0:T(8,128)} %pad_maximum_fusion.2), channel_id=1, source_target_pairs={{1,0},{2,1},{3,2},{4,3},{5,4},{6,5},{7,6},{9,8},{10,9},{11,10},{12... | collective-permute-start | bytes 21233672 | tf_op jit(solution)/shard_map/ppermute | solution.py:19
  912.3 284.2 %collective-permute-start.2 = (f32[3,1,4,384,384]{4,3,2,1,0:T(8,128)}, f32[3,1,4,384,384]{4,3,2,1,0:T(8,128)}, u32[]{:S(2)}, u32[]{:S(2)}) collective-permute-start(f32[3,1,4,384,384]{4,3,2,1,0:T(8,128)} %pad_maximum_fusion.2), channel_id=1, source_target_pairs={{0,1},{1,2},{2,3},{3,4},{4,5},{5,6},{6,7},{8,9},{9,10},{10,11},{11... | collective-permute-start | bytes 21233672 | tf_op jit(solution)/shard_map/ppermute | solution.py:17
  1196.5 2.4 copy-start.5
  1196.5 3.1 copy-start.7
where the time goes:
time: 1230 us; the launch traced here: 1220 us
  waiting for transfers between devices  575 us (47%)
  other arithmetic  412 us (33%)
  local copies, waits for them, and re-layouts  170 us (14%)
  matrix products  40.7 us (3%)
  starting transfers between devices  19.1 us (2%)
    ppermute x2, waiting for transfers between devices, with_halo(): lax.ppermute(head, axis, [((i + 1) % count, i) for i in range(ends)])  281 us
    all_to_all x1, waiting for transfers between devices, body(): lax.all_to_all(outgoing, 'yz', split_axis=0, concat_axis=0, tiled=True)  271 us
    another operation x14, other arithmetic, interpolate(): factor = jnp.linalg.cholesky(gram_rows[:, :, :kept_cols])  225 us
    another operation x5, other arithmetic, interpolate(): jax.scipy.linalg.solve_triangular(factor, half_solved, lower=True, trans=1)  122 us
    gather x1, local copies, waits for them, and re-layouts, body(): pivoted = jnp.take_along_axis(merged, pivots[:, None, :], axis=2)  91.5 us
  transfers between devices with their start and end apart: 5, of which 4 were waited for; matrix products, arithmetic and copies ran while one was open for 0% of the time, Pallas kernels for 0%

commit v1 on v0

v1 whole, which is shorter than its diff:
```python
import functools

import jax
import jax.numpy as jnp
from jax import lax
from jax.experimental import pallas as pl
from jax.experimental.pallas import tpu as pltpu
from jax.sharding import PartitionSpec as P

K = 384
TILE = 128
CHUNKS = 4
HIGHEST = lax.Precision.HIGHEST


def prep_kernel(slot_ref, width_ref, x_ref, o_ref):
    width = width_ref[slot_ref[pl.program_id(0)]]
    lane = lax.broadcasted_iota(jnp.int32, (1, x_ref.shape[2]), 1)
    live = (lane < width).astype(jnp.float32).astype(jnp.bfloat16)
    o_ref[0] = x_ref[0] * live


def pack_outgoing(fine_blocks, source_slot, widths, chunk, rows):
    peers = source_slot.shape[0]
    cols = fine_blocks.shape[2]
    return pl.pallas_call(
        prep_kernel,
        grid_spec=pltpu.PrefetchScalarGridSpec(
            num_scalar_prefetch=2,
            grid=(peers,),
            in_specs=[pl.BlockSpec((1, rows, cols), lambda i, slot, width: (slot[i], chunk, 0))],
            out_specs=pl.BlockSpec((1, rows, cols), lambda i, slot, width: (i, 0, 0)),
        ),
        out_shape=jax.ShapeDtypeStruct((peers, rows, cols), jnp.bfloat16),
        cost_estimate=pl.CostEstimate(
            flops=peers * rows * cols, bytes_accessed=4 * peers * rows * cols, transcendentals=0
        ),
        name=f"pack_{chunk}",
    )(source_slot, widths, fine_blocks)


def gram_kernel(has_prev, first_ref, second_ref, a_ref, b_ref, piv_ref, *refs):
    out_ref = refs[-1]
    cols = a_ref.shape[2]
    piv = piv_ref[0]
    source = lax.broadcasted_iota(jnp.int32, (cols, 2 * cols), 0)
    pick_a = (source == piv).astype(jnp.float32).astype(jnp.bfloat16)
    pick_b = (source + cols == piv).astype(jnp.float32).astype(jnp.bfloat16)
    pivoted = jnp.dot(a_ref[0], pick_a, preferred_element_type=jnp.float32)
    pivoted += jnp.dot(b_ref[0], pick_b, preferred_element_type=jnp.float32)
    pivoted = pivoted.astype(jnp.bfloat16)
    kept = out_ref.shape[1]
    part = lax.dot_general(
        pivoted[:, :kept], pivoted, (((0,), (0,)), ((), ())), preferred_element_type=jnp.float32
    )
    if has_prev:
        out_ref[0] = refs[0][0] + part
    else:
        out_ref[0] = part


def gram_chunk(arrived, first_src, second, pivots, prev, kept_cols):
    _, rows, cols = arrived.shape
    clusters, merged_cols = pivots.shape
    out_spec = pl.BlockSpec((1, kept_cols, merged_cols), lambda c, f, s: (c, 0, 0))
    in_specs = [
        pl.BlockSpec((1, rows, cols), lambda c, f, s: (f[c], 0, 0)),
        pl.BlockSpec((1, rows, cols), lambda c, f, s: (s[c], 0, 0)),
        pl.BlockSpec((1, 1, merged_cols), lambda c, f, s: (c, 0, 0)),
    ]
    operands = [arrived, arrived, pivots.reshape(clusters, 1, merged_cols)]
    aliases = {}
    if prev is not None:
        in_specs.append(out_spec)
        operands.append(prev)
        aliases = {5: 0}
    return pl.pallas_call(
        functools.partial(gram_kernel, prev is not None),
        grid_spec=pltpu.PrefetchScalarGridSpec(
            num_scalar_prefetch=2, grid=(clusters,), in_specs=in_specs, out_specs=out_spec
        ),
        out_shape=jax.ShapeDtypeStruct((clusters, kept_cols, merged_cols), jnp.float32),
        input_output_aliases=aliases,
        cost_estimate=pl.CostEstimate(
            flops=2 * clusters * rows * merged_cols * (merged_cols + kept_cols),
            bytes_accessed=clusters * (4 * rows * cols + 8 * kept_cols * merged_cols),
            transcendentals=0,
        ),
        name="gram_chunk",
    )(first_src, second, *operands)


def factor_kernel(g_ref, x_ref, u_ref, work, inv):
    clusters, kept, cols = g_ref.shape
    panels = kept // TILE
    lane = lax.broadcasted_iota(jnp.int32, (8, TILE), 1)

    def sweep(k, carry):
        is_k = lane == k
        for c in range(clusters):
            a = inv[c]
            row = jnp.broadcast_to(inv[c, pl.ds(k, 1), :], (8, TILE))
            pivot = jnp.take_along_axis(
                row, jnp.full((8, TILE), k, jnp.int32), axis=1, mode="promise_in_bounds"
            )
            col = jnp.take_along_axis(
                a, jnp.full((TILE, TILE), k, jnp.int32), axis=1, mode="promise_in_bounds"
            )
            scaled = (jnp.where(is_k, 1.0, row) / pivot)[:1]
            inv[c] = jnp.where(is_k[:1], 0.0, a) - col * scaled
            inv[c, pl.ds(k, 1), :] = scaled
        return carry

    for p in range(panels):
        src = g_ref if p == 0 else work
        here = slice(p * TILE, (p + 1) * TILE)
        lo = (p + 1) * TILE
        for c in range(clusters):
            inv[c] = src[c, here, here]
        lax.fori_loop(0, TILE, sweep, 0)
        last = p == panels - 1

        def eliminate(c, carry):
            row = jnp.dot(inv[c], src[c, here, lo:], precision=HIGHEST)
            for i in range(panels):
                rows = slice(i * TILE, (i + 1) * TILE)
                if i == p:
                    value = row
                else:
                    value = src[c, rows, lo:] - jnp.dot(src[c, rows, here], row, precision=HIGHEST)
                if last:
                    x_ref[c, rows, :] = value
                else:
                    work[c, rows, lo:] = value
            return carry

        lax.fori_loop(0, clusters, eliminate, 0)

    def outer(c, carry):
        slot = 0
        for i in range(panels):
            left = x_ref[c, i * TILE : (i + 1) * TILE, :]
            part = lax.dot_general(
                left,
                x_ref[c, : (i + 1) * TILE, :],
                (((1,), (1,)), ((), ())),
                precision=HIGHEST,
                preferred_element_type=jnp.float32,
            )
            for j in range(i + 1):
                u_ref[c, slot] = part[:, j * TILE : (j + 1) * TILE]
                slot += 1
        return carry

    lax.fori_loop(0, clusters, outer, 0)


def factor(gram):
    clusters, kept, cols = gram.shape
    panels = kept // TILE
    packed = panels * (panels + 1) // 2
    vmem = pl.BlockSpec(memory_space=pltpu.VMEM)
    return pl.pallas_call(
        factor_kernel,
        in_specs=[vmem],
        out_specs=[vmem, vmem],
        out_shape=[
            jax.ShapeDtypeStruct((clusters, kept, cols - kept), jnp.float32),
            jax.ShapeDtypeStruct((clusters, packed, TILE, TILE), jnp.float32),
        ],
        scratch_shapes=[
            pltpu.VMEM((clusters, kept, cols), jnp.float32),
            pltpu.VMEM((clusters, TILE, TILE), jnp.float32),
        ],
        name="factor",
    )(gram)


def combine_kernel(near_ref, own_ref, *refs):
    out_ref = refs[-1]
    panels = out_ref.shape[1] // TILE
    slot = 0
    for i in range(panels):
        for j in range(i + 1):
            total = own_ref[0, slot]
            for ref in refs[:-1]:
                total = total + ref[0, slot]
            rows = slice(i * TILE, (i + 1) * TILE)
            cols = slice(j * TILE, (j + 1) * TILE)
            out_ref[0, rows, cols] = total
            if i != j:
                out_ref[0, cols, rows] = total.T
            slot += 1


def combine(own, received, neighbours, kept):
    clusters, packed = own.shape[:2]
    block = (1, packed, TILE, TILE)

    def near_spec(side):
        return pl.BlockSpec(block, lambda c, near: (near[4 * c + side], 0, 0, 0))

    return pl.pallas_call(
        combine_kernel,
        grid_spec=pltpu.PrefetchScalarGridSpec(
            num_scalar_prefetch=1,
            grid=(clusters,),
            in_specs=[pl.BlockSpec(block, lambda c, near: (c, 0, 0, 0))]
            + [near_spec(side) for side in range(4)],
            out_specs=pl.BlockSpec((1, kept, kept), lambda c, near: (c, 0, 0)),
        ),
        out_shape=jax.ShapeDtypeStruct((clusters, kept, kept), jnp.float32),
        name="combine",
    )(neighbours.reshape(-1), own, *received)


def exchange(values):
    received = []
    for axis in ("gx", "yz"):
        ends = lax.axis_size(axis) - 1
        received.append(lax.ppermute(values, axis, [(i, i + 1) for i in range(ends)]))
        received.append(lax.ppermute(values, axis, [(i + 1, i) for i in range(ends)]))
    return received


def body(fine_blocks, fine_to_coarse, widths, pivots, neighbours):
    gx_count = lax.axis_size("gx")
    yz_count = lax.axis_size("yz")
    gx_pos = lax.axis_index("gx")
    yz_pos = lax.axis_index("yz")
    blocks_dev, depth, _ = fine_blocks.shape
    clusters = blocks_dev // 2
    device = gx_pos * yz_count + yz_pos
    cluster_table = fine_to_coarse.reshape(gx_count, yz_count, blocks_dev)
    grouped = lax.dynamic_index_in_dim(cluster_table, gx_pos, 0, keepdims=False)
    own_targets = lax.dynamic_index_in_dim(grouped, yz_pos, 0, keepdims=False)
    target = own_targets // clusters - gx_pos * yz_count
    peer_ids = jnp.arange(yz_count, dtype=jnp.int32)
    matches = target[None, :] == peer_ids[:, None]
    source_slot = jnp.sum(
        jnp.where(matches, jnp.arange(blocks_dev, dtype=jnp.int32)[None, :], 0), axis=1
    )
    owned_here = grouped // clusters == device
    member = jnp.any(
        owned_here[None] & ((grouped % clusters)[None] == jnp.arange(clusters)[:, None, None]),
        axis=2,
    )
    first_src = jnp.min(jnp.where(member, peer_ids[None, :], yz_count), axis=1)
    second = jnp.max(jnp.where(member, peer_ids[None, :], -1), axis=1)
    rows = depth // CHUNKS
    gram = None
    for chunk in range(CHUNKS):
        outgoing = pack_outgoing(fine_blocks, source_slot, widths, chunk, rows)
        arrived = lax.all_to_all(outgoing, "yz", split_axis=0, concat_axis=0, tiled=True)
        gram = gram_chunk(arrived, first_src, second, pivots, gram, K)
    interp, packed = factor(gram)
    schur_blocks = combine(packed, exchange(packed), neighbours, K)
    return (interp, schur_blocks)


def solution(mesh):
    return jax.shard_map(
        body,
        mesh=mesh,
        in_specs=(
            P(("gx", "yz"), None, None),
            P(),
            P(("gx", "yz")),
            P(("gx", "yz"), None),
            P(("gx", "yz"), None),
        ),
        out_specs=(P(("gx", "yz"), None, None), P(("gx", "yz"), None, None)),
        check_vma=False,
    )
```

time: 1230 us -> 575 us (0.47)
  other arithmetic: 412 us -> 1.51 us
  waiting for transfers between devices: 575 us -> 294 us
  Pallas kernels: 0 us -> 240 us
  local copies, waits for them, and re-layouts: 170 us -> 6.99 us
  matrix products: 40.7 us -> 0 us
    another operation x20 -> x0, other arithmetic: 351 us -> none  [the longest x14 225 us: interpolate(): factor = jnp.linalg.cholesky(gram_rows[:, :, :kept_cols])]
    pallas_call x0 -> x10, Pallas kernels: none -> 240 us  [the longest x1 167 us: factor(): pl.pallas_call(factor_kernel, in_specs=[vmem], out_specs=[vmem, vmem], ou...]
    ppermute x4, waiting for transfers between devices: 305 us -> 65.1 us  [the longest x2 38.5 us: exchange(): lax.ppermute(values, axis, [(i + 1, i) for i in range(ends)])]
    gather x5 -> x0, local copies, waits for them, and re-layouts: 127 us -> none  [the longest x1 91.5 us: body(): pivoted = jnp.take_along_axis(merged, pivots[:, None, :], axis=2)]
    all_to_all x1 -> x4, waiting for transfers between devices: 271 us -> 228 us  [body(): lax.all_to_all(outgoing, 'yz', split_axis=0, concat_axis=0, tiled=True)]
    another operation x14 -> x0, matrix products: 24.2 us -> none  [the longest x5 10.9 us: interpolate(): jax.scipy.linalg.solve_triangular(factor, gram_rows[:, :, kept_cols:], lo...]
    mul x3 -> x0, other arithmetic: 21.5 us -> none  [the longest x1 10.8 us: body(): outgoing = jnp.take(masked, source_slot, axis=0) * filled[:, None, None]]
    select_n x6 -> x0, other arithmetic: 20.6 us -> none  [the longest x1 10.9 us: body(): pivoted = jnp.take_along_axis(merged, pivots[:, None, :], axis=2)]
  transfers between devices with their start and end apart: 5 -> 8, of which waited for: 4 -> 8; matrix products, arithmetic and copies ran while one was open for 0% -> 0% of each run, Pallas kernels for 0% -> 9%
where the time goes in v1:
time: 575 us; the launch traced here: 574 us
  waiting for transfers between devices  294 us (51%)
  Pallas kernels  240 us (42%)
  starting transfers between devices  31 us (5%)
  local copies, waits for them, and re-layouts  6.99 us (1%)
    all_to_all x4, waiting for transfers between devices, body(): lax.all_to_all(outgoing, 'yz', split_axis=0, concat_axis=0, tiled=True)  228 us
    pallas_call x1, Pallas kernels, factor(): pl.pallas_call(factor_kernel, in_specs=[vmem], out_specs=[vmem, vmem], ou...  167 us
    pallas_call x4, Pallas kernels, gram_chunk(): pl.pallas_call(functools.partial(gram_kernel, prev is not None), grid_spe...  39.4 us
    ppermute x2, waiting for transfers between devices, exchange(): lax.ppermute(values, axis, [(i + 1, i) for i in range(ends)])  38.5 us
    pallas_call x4, Pallas kernels, pack_outgoing(): pl.pallas_call(prep_kernel, grid_spec=pltpu.PrefetchScalarGridSpec(num_sc...  27.4 us
    ppermute x2, waiting for transfers between devices, exchange(): lax.ppermute(values, axis, [(i, i + 1) for i in range(ends)])  26.6 us
    all_to_all x4, starting transfers between devices, body(): lax.all_to_all(outgoing, 'yz', split_axis=0, concat_axis=0, tiled=True)  19.4 us
  transfers between devices with their start and end apart: 8, of which 8 were waited for; matrix products, arithmetic and copies ran while one was open for 0% of the time, Pallas kernels for 9%

profile of v1, /device:TPU:25, one launch (start us, length us, event | category | flops | bytes accessed | tf_op | source)
XLA Modules:
  0.0 573.6 jit_solution(9203747424197748976)
XLA Ops:
  2.0 6.8 %pack_0.1 = bf16[8,384,512]{2,1,0:T(8,128)(2,1)} custom-call(s32[8]{0:T(128)} %select_reduce_fusion.slot_ref, s32[8]{0:T(128)} %width_ref.7, bf16[8,1536,512]{2,1,0:T(8,128)(2,1)} %x_ref.7), custom_call_target="tpu_custom_call" | custom-call | flops 1572864 | bytes 6291456 | tf_op jit(solution)/shard_map/pack_0/pallas_call | solution.py:26
  8.9 5.5 all-to-all-start.3
  14.4 6.8 %pack_1.1 = bf16[8,384,512]{2,1,0:T(8,128)(2,1)} custom-call(s32[8]{0:T(128)} %select_reduce_fusion.slot_ref, s32[8]{0:T(128)} %width_ref.7, bf16[8,1536,512]{2,1,0:T(8,128)(2,1)} %x_ref.7), custom_call_target="tpu_custom_call" | custom-call | flops 1572864 | bytes 6291456 | tf_op jit(solution)/shard_map/pack_1/pallas_call | solution.py:26
  21.2 63.1 %all-to-all-done.3.a_ref.b_ref = bf16[8,384,512]{2,1,0:T(8,128)(2,1)S(1)} async-done(((bf16[8,384,512]{2,1,0:T(8,128)(2,1)}), bf16[8,384,512]{2,1,0:T(8,128)(2,1)S(1)}, u32[]{:S(2)}, u32[]{:S(2)}) %all-to-all-start.3) | async-done | bytes 3145760 | tf_op jit(solution)/shard_map/all_to_all | solution.py:254
  85.9 4.6 all-to-all-start.2
  90.5 6.9 %pack_2.1 = bf16[8,384,512]{2,1,0:T(8,128)(2,1)} custom-call(s32[8]{0:T(128)} %select_reduce_fusion.slot_ref, s32[8]{0:T(128)} %width_ref.7, bf16[8,1536,512]{2,1,0:T(8,128)(2,1)} %x_ref.7), custom_call_target="tpu_custom_call" | custom-call | flops 1572864 | bytes 6291456 | tf_op jit(solution)/shard_map/pack_2/pallas_call | solution.py:26
  97.4 63.1 %all-to-all-done.2.a_ref.b_ref = bf16[8,384,512]{2,1,0:T(8,128)(2,1)S(1)} async-done(((bf16[8,384,512]{2,1,0:T(8,128)(2,1)}), bf16[8,384,512]{2,1,0:T(8,128)(2,1)S(1)}, u32[]{:S(2)}, u32[]{:S(2)}) %all-to-all-start.2) | async-done | bytes 3145760 | tf_op jit(solution)/shard_map/all_to_all | solution.py:254
  162.1 4.6 all-to-all-start.1
  166.7 6.8 %pack_3.1 = bf16[8,384,512]{2,1,0:T(8,128)(2,1)} custom-call(s32[8]{0:T(128)} %select_reduce_fusion.slot_ref, s32[8]{0:T(128)} %width_ref.7, bf16[8,1536,512]{2,1,0:T(8,128)(2,1)} %x_ref.7), custom_call_target="tpu_custom_call" | custom-call | flops 1572864 | bytes 6291456 | tf_op jit(solution)/shard_map/pack_3/pallas_call | solution.py:26
  173.6 63.2 %all-to-all-done.1.a_ref.b_ref = bf16[8,384,512]{2,1,0:T(8,128)(2,1)} async-done(((bf16[8,384,512]{2,1,0:T(8,128)(2,1)}), bf16[8,384,512]{2,1,0:T(8,128)(2,1)}, u32[]{:S(2)}, u32[]{:S(2)}) %all-to-all-start.1) | async-done | bytes 3145760 | tf_op jit(solution)/shard_map/all_to_all | solution.py:254
  236.7 4.6 all-to-all-start
  242.9 8.9 %gram_chunk.4.refs_0_ = f32[4,384,1024]{2,1,0:T(8,128)} custom-call(s32[4]{0:T(128)} %get-tuple-element.7.first_ref, s32[4]{0:T(128)} %get-tuple-element.6.second_ref, bf16[8,384,512]{2,1,0:T(8,128)(2,1)} %copy-done.2, bf16[8,384,512]{2,1,0:T(8,128)(2,1)} %copy-done.2, s32[4,1,1024]{2,1,0:T(1,128)} %reshape.48.piv_ref), custom_call_target="tpu_custom_call" | custom-call | flops 4429185024 | bytes 15728640 | tf_op jit(solution)/shard_map/gram_chunk/pallas_call | solution.py:77
  251.8 10.2 %gram_chunk.5.refs_0_ = f32[4,384,1024]{2,1,0:T(8,128)} custom-call(s32[4]{0:T(128)} %get-tuple-element.7.first_ref, s32[4]{0:T(128)} %get-tuple-element.6.second_ref, bf16[8,384,512]{2,1,0:T(8,128)(2,1)} %copy-done, bf16[8,384,512]{2,1,0:T(8,128)(2,1)} %copy-done, s32[4,1,1024]{2,1,0:T(1,128)} %reshape.48.piv_ref, ...), custom_call_target="tpu_custom_call", output_to_operand_aliasing={{}: (5, {})} | custom-call | flops 4429185024 | bytes 15728640 | tf_op jit(solution)/shard_map/gram_chunk/pallas_call | solution.py:77
  262.0 10.2 %gram_chunk.6.refs_0_ = f32[4,384,1024]{2,1,0:T(8,128)} custom-call(s32[4]{0:T(128)} %get-tuple-element.7.first_ref, s32[4]{0:T(128)} %get-tuple-element.6.second_ref, bf16[8,384,512]{2,1,0:T(8,128)(2,1)} %all-to-all-done.1.a_ref.b_ref, bf16[8,384,512]{2,1,0:T(8,128)(2,1)} %all-to-all-done.1.a_ref.b_ref, ...), custom_call_target="tpu_custom_call", output_to_operand_aliasing={{}: (5, {})} | custom-call | flops 4429185024 | bytes 15728640 | tf_op jit(solution)/shard_map/gram_chunk/pallas_call | solution.py:77
  272.1 39.1 %all-to-all-done.a_ref.b_ref = bf16[8,384,512]{2,1,0:T(8,128)(2,1)S(1)} async-done(((bf16[8,384,512]{2,1,0:T(8,128)(2,1)}), bf16[8,384,512]{2,1,0:T(8,128)(2,1)S(1)}, u32[]{:S(2)}, u32[]{:S(2)}) %all-to-all-start) | async-done | bytes 3145760 | tf_op jit(solution)/shard_map/all_to_all | solution.py:254
  312.9 10.2 %gram_chunk.7.g_ref = f32[4,384,1024]{2,1,0:T(8,128)} custom-call(s32[4]{0:T(128)} %get-tuple-element.7.first_ref, s32[4]{0:T(128)} %get-tuple-element.6.second_ref, bf16[8,384,512]{2,1,0:T(8,128)(2,1)} %copy-done.1, bf16[8,384,512]{2,1,0:T(8,128)(2,1)} %copy-done.1, s32[4,1,1024]{2,1,0:T(1,128)} %reshape.48.piv_ref, ...), custom_call_target="tpu_custom_call", output_to_operand_aliasing={{}: (5, {})} | custom-call | flops 4429185024 | bytes 15728640 | tf_op jit(solution)/shard_map/gram_chunk/pallas_call | solution.py:77
  323.1 167.3 %factor.1 = (f32[4,384,640]{2,1,0:T(8,128)}, f32[4,6,128,128]{3,2,1,0:T(8,128)}) custom-call(f32[4,384,1024]{2,1,0:T(8,128)} %gram_chunk.7.g_ref), custom_call_target="tpu_custom_call" | custom-call | tf_op jit(solution)/shard_map/factor/pallas_call | solution.py:163
  490.4 3.5 collective-permute-start
  498.1 3.9 collective-permute-start.3
  502.7 8.9 %collective-permute-done.refs_0_ = f32[4,6,128,128]{3,2,1,0:T(8,128)S(1)} collective-permute-done((f32[4,6,128,128]{3,2,1,0:T(8,128)}, f32[4,6,128,128]{3,2,1,0:T(8,128)S(1)}, u32[]{:S(2)}, u32[]{:S(2)}) %collective-permute-start) | collective-permute-done | bytes 1572896 | tf_op jit(solution)/shard_map/ppermute | solution.py:221
  511.6 4.7 collective-permute-done.1.refs_1_
  516.3 17.8 %collective-permute-done.2.refs_2_ = f32[4,6,128,128]{3,2,1,0:T(8,128)} collective-permute-done((f32[4,6,128,128]{3,2,1,0:T(8,128)}, f32[4,6,128,128]{3,2,1,0:T(8,128)}, u32[]{:S(2)}, u32[]{:S(2)}) %collective-permute-start.2) | collective-permute-done | bytes 1572896 | tf_op jit(solution)/shard_map/ppermute | solution.py:221
  534.0 33.8 %collective-permute-done.3.refs_3_ = f32[4,6,128,128]{3,2,1,0:T(8,128)} collective-permute-done((f32[4,6,128,128]{3,2,1,0:T(8,128)}, f32[4,6,128,128]{3,2,1,0:T(8,128)}, u32[]{:S(2)}, u32[]{:S(2)}) %collective-permute-start.3) | collective-permute-done | bytes 1572896 | tf_op jit(solution)/shard_map/ppermute | solution.py:222
  567.9 5.7 combine.1
  (25 shorter events, 12.7 us)
Async XLA Ops:
  8.9 75.4 %all-to-all-start.3 = ((bf16[8,384,512]{2,1,0:T(8,128)(2,1)}), bf16[8,384,512]{2,1,0:T(8,128)(2,1)S(1)}, u32[]{:S(2)}, u32[]{:S(2)}) async-start(bf16[8,384,512]{2,1,0:T(8,128)(2,1)} %pack_0.1), calls=%async_computation.3 | async-start | bytes 6291456 | tf_op jit(solution)/shard_map/all_to_all | solution.py:254
  84.3 1.6 copy-start.2
  85.9 74.5 %all-to-all-start.2 = ((bf16[8,384,512]{2,1,0:T(8,128)(2,1)}), bf16[8,384,512]{2,1,0:T(8,128)(2,1)S(1)}, u32[]{:S(2)}, u32[]{:S(2)}) async-start(bf16[8,384,512]{2,1,0:T(8,128)(2,1)} %pack_1.1), calls=%async_computation.2 | async-start | bytes 6291456 | tf_op jit(solution)/shard_map/all_to_all | solution.py:254
  160.5 1.7 copy-start
  162.1 74.6 %all-to-all-start.1 = ((bf16[8,384,512]{2,1,0:T(8,128)(2,1)}), bf16[8,384,512]{2,1,0:T(8,128)(2,1)}, u32[]{:S(2)}, u32[]{:S(2)}) async-start(bf16[8,384,512]{2,1,0:T(8,128)(2,1)} %pack_2.1), calls=%async_computation.1 | async-start | bytes 6291456 | tf_op jit(solution)/shard_map/all_to_all | solution.py:254
  173.6 67.8 %copy-start.5 = (s32[4,1024]{1,0:T(4,128)S(1)}, s32[4,1024]{1,0:T(4,128)}, u32[]{:S(2)}) copy-start(s32[4,1024]{1,0:T(4,128)} %param.8) | copy-start | bytes 49156
  236.7 74.5 %all-to-all-start = ((bf16[8,384,512]{2,1,0:T(8,128)(2,1)}), bf16[8,384,512]{2,1,0:T(8,128)(2,1)S(1)}, u32[]{:S(2)}, u32[]{:S(2)}) async-start(bf16[8,384,512]{2,1,0:T(8,128)(2,1)} %pack_3.1), calls=%async_computation | async-start | bytes 6291456 | tf_op jit(solution)/shard_map/all_to_all | solution.py:254
  311.3 1.7 copy-start.1
  323.1 179.0 %copy-start.6 = (s32[4,4]{1,0:T(4,128)S(1)}, s32[4,4]{1,0:T(4,128)}, u32[]{:S(2)}) copy-start(s32[4,4]{1,0:T(4,128)} %param.9) | copy-start | bytes 196
  490.4 21.1 %collective-permute-start = (f32[4,6,128,128]{3,2,1,0:T(8,128)}, f32[4,6,128,128]{3,2,1,0:T(8,128)S(1)}, u32[]{:S(2)}, u32[]{:S(2)}) collective-permute-start(f32[4,6,128,128]{3,2,1,0:T(8,128)} %get-tuple-element.5.own_ref), channel_id=1, source_target_pairs={{0,8},{8,16},{16,24},{1,9},{9,17},{17,25},{2,10},{10,18},{18,26},{... | collective-permute-start | bytes 4718600 | tf_op jit(solution)/shard_map/ppermute | solution.py:221
  493.9 22.3 %collective-permute-start.1 = (f32[4,6,128,128]{3,2,1,0:T(8,128)}, f32[4,6,128,128]{3,2,1,0:T(8,128)S(1)}, u32[]{:S(2)}, u32[]{:S(2)}) collective-permute-start(f32[4,6,128,128]{3,2,1,0:T(8,128)} %get-tuple-element.5.own_ref), channel_id=1, source_target_pairs={{8,0},{16,8},{24,16},{9,1},{17,9},{25,17},{10,2},{18,10},{26,18},{... | collective-permute-start | bytes 4718600 | tf_op jit(solution)/shard_map/ppermute | solution.py:222
  495.9 38.2 %collective-permute-start.2 = (f32[4,6,128,128]{3,2,1,0:T(8,128)}, f32[4,6,128,128]{3,2,1,0:T(8,128)}, u32[]{:S(2)}, u32[]{:S(2)}) collective-permute-start(f32[4,6,128,128]{3,2,1,0:T(8,128)} %get-tuple-element.5.own_ref), channel_id=1, source_target_pairs={{0,1},{1,2},{2,3},{3,4},{4,5},{5,6},{6,7},{8,9},{9,10},{10,11},{11... | collective-permute-start | bytes 4718600 | tf_op jit(solution)/shard_map/ppermute | solution.py:221
  498.1 69.7 %collective-permute-start.3 = (f32[4,6,128,128]{3,2,1,0:T(8,128)}, f32[4,6,128,128]{3,2,1,0:T(8,128)}, u32[]{:S(2)}, u32[]{:S(2)}) collective-permute-start(f32[4,6,128,128]{3,2,1,0:T(8,128)} %get-tuple-element.5.own_ref), channel_id=1, source_target_pairs={{1,0},{2,1},{3,2},{4,3},{5,4},{6,5},{7,6},{9,8},{10,9},{11,10},{12... | collective-permute-start | bytes 4718600 | tf_op jit(solution)/shard_map/ppermute | solution.py:222
  511.6 56.3 %copy-start.3 = (f32[4,6,128,128]{3,2,1,0:T(8,128)}, f32[4,6,128,128]{3,2,1,0:T(8,128)S(1)}, u32[]{:S(2)}) copy-start(f32[4,6,128,128]{3,2,1,0:T(8,128)S(1)} %collective-permute-done.refs_0_) | copy-start | bytes 4718596
  516.3 51.6 %copy-start.4 = (f32[4,6,128,128]{3,2,1,0:T(8,128)}, f32[4,6,128,128]{3,2,1,0:T(8,128)S(1)}, u32[]{:S(2)}) copy-start(f32[4,6,128,128]{3,2,1,0:T(8,128)S(1)} %collective-permute-done.1.refs_1_) | copy-start | bytes 4718596

commit v2 on v1

--- a/solution.py
+++ b/solution.py
@@ -9,7 +9,7 @@
 
 K = 384
 TILE = 128
-CHUNKS = 4
+CHUNKS = (1, 2, 1)
 HIGHEST = lax.Precision.HIGHEST
 
 
@@ -20,22 +20,23 @@
     o_ref[0] = x_ref[0] * live
 
 
-def pack_outgoing(fine_blocks, source_slot, widths, chunk, rows):
+def pack_outgoing(fine_blocks, source_slot, widths, first, count, rows):
     peers = source_slot.shape[0]
     cols = fine_blocks.shape[2]
+    total = peers * count * rows * cols
     return pl.pallas_call(
         prep_kernel,
         grid_spec=pltpu.PrefetchScalarGridSpec(
             num_scalar_prefetch=2,
-            grid=(peers,),
-            in_specs=[pl.BlockSpec((1, rows, cols), lambda i, slot, width: (slot[i], chunk, 0))],
-            out_specs=pl.BlockSpec((1, rows, cols), lambda i, slot, width: (i, 0, 0)),
-        ),
-        out_shape=jax.ShapeDtypeStruct((peers, rows, cols), jnp.bfloat16),
-        cost_estimate=pl.CostEstimate(
-            flops=peers * rows * cols, bytes_accessed=4 * peers * rows * cols, transcendentals=0
-        ),
-        name=f"pack_{chunk}",
+            grid=(peers, count),
+            in_specs=[
+                pl.BlockSpec((1, rows, cols), lambda i, j, slot, width: (slot[i], first + j, 0))
+            ],
+            out_specs=pl.BlockSpec((1, rows, cols), lambda i, j, slot, width: (i, j, 0)),
+        ),
+        out_shape=jax.ShapeDtypeStruct((peers, count * rows, cols), jnp.bfloat16),
+        cost_estimate=pl.CostEstimate(flops=total, bytes_accessed=4 * total, transcendentals=0),
+        name=f"pack_{first}",
     )(source_slot, widths, fine_blocks)
 
 
@@ -93,23 +94,51 @@
 def factor_kernel(g_ref, x_ref, u_ref, work, inv):
     clusters, kept, cols = g_ref.shape
     panels = kept // TILE
-    lane = lax.broadcasted_iota(jnp.int32, (8, TILE), 1)
-
-    def sweep(k, carry):
-        is_k = lane == k
+    sub = TILE // clusters
+    lane = lax.broadcasted_iota(jnp.int32, (sub, TILE), 1)
+    row_id = lax.broadcasted_iota(jnp.int32, (sub, TILE), 0)
+    segment = lane // sub
+    offset = lane - segment * sub
+    wide_segment = lax.broadcasted_iota(jnp.int32, (TILE, TILE), 1) // sub
+
+    def invert_small(a):
+        for k in range(sub):
+            index = segment * sub + k
+            col = jnp.take_along_axis(a, index, axis=1, mode="promise_in_bounds")
+            row = jnp.broadcast_to(a[k : k + 1, :], (sub, TILE))
+            pivot = jnp.broadcast_to(col[k : k + 1, :], (sub, TILE))
+            is_k = offset == k
+            scaled = jnp.where(is_k, 1.0, row) / pivot
+            a = jnp.where(row_id == k, scaled, jnp.where(is_k, 0.0, a) - col * scaled)
+        return a
+
+    def invert_block(q):
+        here = slice(q * sub, (q + 1) * sub)
+        small = jnp.zeros((sub, TILE), jnp.float32)
         for c in range(clusters):
-            a = inv[c]
-            row = jnp.broadcast_to(inv[c, pl.ds(k, 1), :], (8, TILE))
-            pivot = jnp.take_along_axis(
-                row, jnp.full((8, TILE), k, jnp.int32), axis=1, mode="promise_in_bounds"
-            )
-            col = jnp.take_along_axis(
-                a, jnp.full((TILE, TILE), k, jnp.int32), axis=1, mode="promise_in_bounds"
-            )
-            scaled = (jnp.where(is_k, 1.0, row) / pivot)[:1]
-            inv[c] = jnp.where(is_k[:1], 0.0, a) - col * scaled
-            inv[c, pl.ds(k, 1), :] = scaled
-        return carry
+            moved = inv[c, here, :]
+            if c != q:
+                moved = pltpu.roll(moved, ((c - q) * sub) % TILE, 1)
+            small = jnp.where(segment == c, moved, small)
+        small = invert_small(small)
+        for c in range(clusters):
+            block = inv[c]
+            moved = small
+            if c != q:
+                moved = pltpu.roll(small, ((q - c) * sub) % TILE, 1)
+            pivot_inv = jnp.where(segment == q, moved, 0.0)
+            row = jnp.dot(pivot_inv, block, precision=HIGHEST)
+            row = jnp.where(segment == q, moved, row)
+            parts = [row]
+            if q > 0:
+                parts.insert(0, jnp.zeros((q * sub, TILE), jnp.float32))
+            if q < clusters - 1:
+                parts.append(jnp.zeros(((clusters - 1 - q) * sub, TILE), jnp.float32))
+            padded = jnp.concatenate(parts, axis=0)
+            in_q = wide_segment == q
+            step = jnp.dot(jnp.where(in_q, block, 0.0), padded, precision=HIGHEST)
+            inv[c] = jnp.where(in_q, 0.0, block) - step
+            inv[c, here, :] = row
 
     for p in range(panels):
         src = g_ref if p == 0 else work
@@ -117,7 +146,8 @@
         lo = (p + 1) * TILE
         for c in range(clusters):
             inv[c] = src[c, here, here]
-        lax.fori_loop(0, TILE, sweep, 0)
+        for q in range(clusters):
+            invert_block(q)
         last = p == panels - 1
 
         def eliminate(c, carry):
@@ -247,10 +277,12 @@
     )
     first_src = jnp.min(jnp.where(member, peer_ids[None, :], yz_count), axis=1)
     second = jnp.max(jnp.where(member, peer_ids[None, :], -1), axis=1)
-    rows = depth // CHUNKS
+    rows = depth // sum(CHUNKS)
     gram = None
-    for chunk in range(CHUNKS):
-        outgoing = pack_outgoing(fine_blocks, source_slot, widths, chunk, rows)
+    first = 0
+    for count in CHUNKS:
+        outgoing = pack_outgoing(fine_blocks, source_slot, widths, first, count, rows)
+        first += count
         arrived = lax.all_to_all(outgoing, "yz", split_axis=0, concat_axis=0, tiled=True)
         gram = gram_chunk(arrived, first_src, second, pivots, gram, K)
     interp, packed = factor(gram)

time: 575 us -> 473 us (0.82)
  Pallas kernels: 240 us -> 138 us
  waiting for transfers between devices: 294 us -> 300 us
    pallas_call x1, Pallas kernels: 167 us -> 73.9 us  [factor(): pl.pallas_call(factor_kernel, in_specs=[vmem], out_specs=[vmem, vmem], ou...]
    pallas_call x4 -> x3, Pallas kernels: 39.4 us -> 32.8 us  [gram_chunk(): pl.pallas_call(functools.partial(gram_kernel, prev is not None), grid_spe...]
    all_to_all x4 -> x3, waiting for transfers between devices: 228 us -> 234 us  [body(): lax.all_to_all(outgoing, 'yz', split_axis=0, concat_axis=0, tiled=True)]
    all_to_all x4 -> x3, starting transfers between devices: 19.4 us -> 14.7 us  [body(): lax.all_to_all(outgoing, 'yz', split_axis=0, concat_axis=0, tiled=True)]
    pallas_call x4 -> x3, Pallas kernels: 27.4 us -> 25.4 us  [pack_outgoing(): pl.pallas_call(prep_kernel, grid_spec=pltpu.PrefetchScalarGridSpec(num_sc...]
  transfers between devices with their start and end apart: 8 -> 7, of which waited for: 8 -> 7; matrix products, arithmetic and copies ran while one was open for 0% -> 0% of each run, Pallas kernels for 9% -> 9%
where the time goes in v2:
time: 473 us; the launch traced here: 471 us
  waiting for transfers between devices  300 us (63%)
  Pallas kernels  138 us (29%)
  starting transfers between devices  26.3 us (6%)
  local copies, waits for them, and re-layouts  5.26 us (1%)
    all_to_all x3, waiting for transfers between devices, body(): lax.all_to_all(outgoing, 'yz', split_axis=0, concat_axis=0, tiled=True)  234 us
    pallas_call x1, Pallas kernels, factor(): pl.pallas_call(factor_kernel, in_specs=[vmem], out_specs=[vmem, vmem], ou...  73.9 us
    ppermute x2, waiting for transfers between devices, exchange(): lax.ppermute(values, axis, [(i + 1, i) for i in range(ends)])  38.5 us
    pallas_call x3, Pallas kernels, gram_chunk(): pl.pallas_call(functools.partial(gram_kernel, prev is not None), grid_spe...  32.8 us
    ppermute x2, waiting for transfers between devices, exchange(): lax.ppermute(values, axis, [(i, i + 1) for i in range(ends)])  26.7 us
    pallas_call x3, Pallas kernels, pack_outgoing(): pl.pallas_call(prep_kernel, grid_spec=pltpu.PrefetchScalarGridSpec(num_sc...  25.4 us
    all_to_all x3, starting transfers between devices, body(): lax.all_to_all(outgoing, 'yz', split_axis=0, concat_axis=0, tiled=True)  14.7 us
  transfers between devices with their start and end apart: 7, of which 7 were waited for; matrix products, arithmetic and copies ran while one was open for 0% of the time, Pallas kernels for 9%

profile of v2, /device:TPU:25, one launch (start us, length us, event | category | flops | bytes accessed | tf_op | source)
XLA Modules:
  0.0 471.3 jit_solution(7772069590238459119)
XLA Ops:
  2.0 6.8 %pack_0.1 = bf16[8,384,512]{2,1,0:T(8,128)(2,1)} custom-call(s32[8]{0:T(128)} %select_reduce_fusion.slot_ref, s32[8]{0:T(128)} %width_ref.5, bf16[8,1536,512]{2,1,0:T(8,128)(2,1)} %x_ref.5), custom_call_target="tpu_custom_call" | custom-call | flops 1572864 | bytes 6291456 | tf_op jit(solution)/shard_map/pack_0/pallas_call | solution.py:27
  8.9 5.5 %all-to-all-start.2 = ((bf16[8,384,512]{2,1,0:T(8,128)(2,1)}), bf16[8,384,512]{2,1,0:T(8,128)(2,1)S(1)}, u32[]{:S(2)}, u32[]{:S(2)}) async-start(bf16[8,384,512]{2,1,0:T(8,128)(2,1)} %pack_0.1), calls=%async_computation.2 | async-start | bytes 6291456 | tf_op jit(solution)/shard_map/all_to_all | solution.py:286
  14.4 11.7 %pack_1.1 = bf16[8,768,512]{2,1,0:T(8,128)(2,1)} custom-call(s32[8]{0:T(128)} %select_reduce_fusion.slot_ref, s32[8]{0:T(128)} %width_ref.5, bf16[8,1536,512]{2,1,0:T(8,128)(2,1)} %x_ref.5), custom_call_target="tpu_custom_call" | custom-call | flops 3145728 | bytes 12582912 | tf_op jit(solution)/shard_map/pack_1/pallas_call | solution.py:27
  26.1 58.2 %all-to-all-done.2.a_ref.b_ref = bf16[8,384,512]{2,1,0:T(8,128)(2,1)S(1)} async-done(((bf16[8,384,512]{2,1,0:T(8,128)(2,1)}), bf16[8,384,512]{2,1,0:T(8,128)(2,1)S(1)}, u32[]{:S(2)}, u32[]{:S(2)}) %all-to-all-start.2) | async-done | bytes 3145760 | tf_op jit(solution)/shard_map/all_to_all | solution.py:286
  84.3 1.6 copy-done.1
  85.9 4.7 %all-to-all-start.1 = ((bf16[8,768,512]{2,1,0:T(8,128)(2,1)}), bf16[8,768,512]{2,1,0:T(8,128)(2,1)}, u32[]{:S(2)}, u32[]{:S(2)}) async-start(bf16[8,768,512]{2,1,0:T(8,128)(2,1)} %pack_1.1), calls=%async_computation.1 | async-start | bytes 12582912 | tf_op jit(solution)/shard_map/all_to_all | solution.py:286
  90.7 6.8 %pack_3.1 = bf16[8,384,512]{2,1,0:T(8,128)(2,1)} custom-call(s32[8]{0:T(128)} %select_reduce_fusion.slot_ref, s32[8]{0:T(128)} %width_ref.5, bf16[8,1536,512]{2,1,0:T(8,128)(2,1)} %x_ref.5), custom_call_target="tpu_custom_call" | custom-call | flops 1572864 | bytes 6291456 | tf_op jit(solution)/shard_map/pack_3/pallas_call | solution.py:27
  97.5 130.5 %all-to-all-done.1.a_ref.b_ref = bf16[8,768,512]{2,1,0:T(8,128)(2,1)} async-done(((bf16[8,768,512]{2,1,0:T(8,128)(2,1)}), bf16[8,768,512]{2,1,0:T(8,128)(2,1)}, u32[]{:S(2)}, u32[]{:S(2)}) %all-to-all-start.1) | async-done | bytes 6291488 | tf_op jit(solution)/shard_map/all_to_all | solution.py:286
  228.0 4.5 all-to-all-start
  234.0 8.9 %gram_chunk.3.refs_0_ = f32[4,384,1024]{2,1,0:T(8,128)} custom-call(s32[4]{0:T(128)} %get-tuple-element.7.first_ref, s32[4]{0:T(128)} %get-tuple-element.6.second_ref, bf16[8,384,512]{2,1,0:T(8,128)(2,1)} %copy-done.1, bf16[8,384,512]{2,1,0:T(8,128)(2,1)} %copy-done.1, s32[4,1,1024]{2,1,0:T(1,128)} %reshape.47.piv_ref), custom_call_target="tpu_custom_call" | custom-call | flops 4429185024 | bytes 15728640 | tf_op jit(solution)/shard_map/gram_chunk/pallas_call | solution.py:78
  243.0 13.7 %gram_chunk.4.refs_0_ = f32[4,384,1024]{2,1,0:T(8,128)} custom-call(s32[4]{0:T(128)} %get-tuple-element.7.first_ref, s32[4]{0:T(128)} %get-tuple-element.6.second_ref, bf16[8,768,512]{2,1,0:T(8,128)(2,1)} %all-to-all-done.1.a_ref.b_ref, bf16[8,768,512]{2,1,0:T(8,128)(2,1)} %all-to-all-done.1.a_ref.b_ref, ...), custom_call_target="tpu_custom_call", output_to_operand_aliasing={{}: (5, {})} | custom-call | flops 8858370048 | bytes 18874368 | tf_op jit(solution)/shard_map/gram_chunk/pallas_call | solution.py:78
  256.7 45.8 %all-to-all-done.a_ref.b_ref = bf16[8,384,512]{2,1,0:T(8,128)(2,1)S(1)} async-done(((bf16[8,384,512]{2,1,0:T(8,128)(2,1)}), bf16[8,384,512]{2,1,0:T(8,128)(2,1)S(1)}, u32[]{:S(2)}, u32[]{:S(2)}) %all-to-all-start) | async-done | bytes 3145760 | tf_op jit(solution)/shard_map/all_to_all | solution.py:286
  302.4 1.7 copy-done
  304.1 10.2 %gram_chunk.5.g_ref = f32[4,384,1024]{2,1,0:T(8,128)} custom-call(s32[4]{0:T(128)} %get-tuple-element.7.first_ref, s32[4]{0:T(128)} %get-tuple-element.6.second_ref, bf16[8,384,512]{2,1,0:T(8,128)(2,1)} %copy-done, bf16[8,384,512]{2,1,0:T(8,128)(2,1)} %copy-done, s32[4,1,1024]{2,1,0:T(1,128)} %reshape.47.piv_ref, ...), custom_call_target="tpu_custom_call", output_to_operand_aliasing={{}: (5, {})} | custom-call | flops 4429185024 | bytes 15728640 | tf_op jit(solution)/shard_map/gram_chunk/pallas_call | solution.py:78
  314.3 73.9 %factor.1 = (f32[4,384,640]{2,1,0:T(8,128)}, f32[4,6,128,128]{3,2,1,0:T(8,128)}) custom-call(f32[4,384,1024]{2,1,0:T(8,128)} %gram_chunk.5.g_ref), custom_call_target="tpu_custom_call" | custom-call | tf_op jit(solution)/shard_map/factor/pallas_call | solution.py:193
  388.1 3.5 collective-permute-start
  391.6 1.9 collective-permute-start.1
  393.6 2.3 collective-permute-start.2
  395.8 3.9 collective-permute-start.3
  400.3 9.0 %collective-permute-done.refs_0_ = f32[4,6,128,128]{3,2,1,0:T(8,128)S(1)} collective-permute-done((f32[4,6,128,128]{3,2,1,0:T(8,128)}, f32[4,6,128,128]{3,2,1,0:T(8,128)S(1)}, u32[]{:S(2)}, u32[]{:S(2)}) %collective-permute-start) | collective-permute-done | bytes 1572896 | tf_op jit(solution)/shard_map/ppermute | solution.py:251
  409.3 4.7 collective-permute-done.1.refs_1_
  414.0 17.8 %collective-permute-done.2.refs_2_ = f32[4,6,128,128]{3,2,1,0:T(8,128)} collective-permute-done((f32[4,6,128,128]{3,2,1,0:T(8,128)}, f32[4,6,128,128]{3,2,1,0:T(8,128)}, u32[]{:S(2)}, u32[]{:S(2)}) %collective-permute-start.2) | collective-permute-done | bytes 1572896 | tf_op jit(solution)/shard_map/ppermute | solution.py:251
  431.7 33.8 %collective-permute-done.3.refs_3_ = f32[4,6,128,128]{3,2,1,0:T(8,128)} collective-permute-done((f32[4,6,128,128]{3,2,1,0:T(8,128)}, f32[4,6,128,128]{3,2,1,0:T(8,128)}, u32[]{:S(2)}, u32[]{:S(2)}) %collective-permute-start.3) | collective-permute-done | bytes 1572896 | tf_op jit(solution)/shard_map/ppermute | solution.py:252
  465.6 5.7 %combine.1 = f32[4,384,384]{2,1,0:T(8,128)} custom-call(s32[16]{0:T(128)} %reshape.48.near_ref, f32[4,6,128,128]{3,2,1,0:T(8,128)} %get-tuple-element.5.own_ref, f32[4,6,128,128]{3,2,1,0:T(8,128)} %copy-done.2, f32[4,6,128,128]{3,2,1,0:T(8,128)} %copy-done.3, f32[4,6,128,128]{3,2,1,0:T(8,128)} %collective-permute-done.2.refs_2_, ...), custom_call_target="tpu_custom_call" | custom-call | tf_op jit(solution)/shard_map/combine/pallas_call | solution.py:233
  (19 shorter events, 3.5 us)
Async XLA Ops:
  8.9 75.4 %all-to-all-start.2 = ((bf16[8,384,512]{2,1,0:T(8,128)(2,1)}), bf16[8,384,512]{2,1,0:T(8,128)(2,1)S(1)}, u32[]{:S(2)}, u32[]{:S(2)}) async-start(bf16[8,384,512]{2,1,0:T(8,128)(2,1)} %pack_0.1), calls=%async_computation.2 | async-start | bytes 6291456 | tf_op jit(solution)/shard_map/all_to_all | solution.py:286
  84.3 1.6 copy-start.1
  85.9 142.1 %all-to-all-start.1 = ((bf16[8,768,512]{2,1,0:T(8,128)(2,1)}), bf16[8,768,512]{2,1,0:T(8,128)(2,1)}, u32[]{:S(2)}, u32[]{:S(2)}) async-start(bf16[8,768,512]{2,1,0:T(8,128)(2,1)} %pack_1.1), calls=%async_computation.1 | async-start | bytes 12582912 | tf_op jit(solution)/shard_map/all_to_all | solution.py:286
  97.5 135.0 %copy-start.4 = (s32[4,1024]{1,0:T(4,128)S(1)}, s32[4,1024]{1,0:T(4,128)}, u32[]{:S(2)}) copy-start(s32[4,1024]{1,0:T(4,128)} %param.8) | copy-start | bytes 49156
  228.0 74.4 %all-to-all-start = ((bf16[8,384,512]{2,1,0:T(8,128)(2,1)}), bf16[8,384,512]{2,1,0:T(8,128)(2,1)S(1)}, u32[]{:S(2)}, u32[]{:S(2)}) async-start(bf16[8,384,512]{2,1,0:T(8,128)(2,1)} %pack_3.1), calls=%async_computation | async-start | bytes 6291456 | tf_op jit(solution)/shard_map/all_to_all | solution.py:286
  302.4 1.7 copy-start
  314.3 85.5 %copy-start.5 = (s32[4,4]{1,0:T(4,128)S(1)}, s32[4,4]{1,0:T(4,128)}, u32[]{:S(2)}) copy-start(s32[4,4]{1,0:T(4,128)} %param.9) | copy-start | bytes 196
  388.1 21.1 %collective-permute-start = (f32[4,6,128,128]{3,2,1,0:T(8,128)}, f32[4,6,128,128]{3,2,1,0:T(8,128)S(1)}, u32[]{:S(2)}, u32[]{:S(2)}) collective-permute-start(f32[4,6,128,128]{3,2,1,0:T(8,128)} %get-tuple-element.5.own_ref), channel_id=1, source_target_pairs={{0,8},{8,16},{16,24},{1,9},{9,17},{17,25},{2,10},{10,18},{18,26},{... | collective-permute-start | bytes 4718600 | tf_op jit(solution)/shard_map/ppermute | solution.py:251
  391.6 22.3 %collective-permute-start.1 = (f32[4,6,128,128]{3,2,1,0:T(8,128)}, f32[4,6,128,128]{3,2,1,0:T(8,128)S(1)}, u32[]{:S(2)}, u32[]{:S(2)}) collective-permute-start(f32[4,6,128,128]{3,2,1,0:T(8,128)} %get-tuple-element.5.own_ref), channel_id=1, source_target_pairs={{8,0},{16,8},{24,16},{9,1},{17,9},{25,17},{10,2},{18,10},{26,18},{... | collective-permute-start | bytes 4718600 | tf_op jit(solution)/shard_map/ppermute | solution.py:252
  393.6 38.2 %collective-permute-start.2 = (f32[4,6,128,128]{3,2,1,0:T(8,128)}, f32[4,6,128,128]{3,2,1,0:T(8,128)}, u32[]{:S(2)}, u32[]{:S(2)}) collective-permute-start(f32[4,6,128,128]{3,2,1,0:T(8,128)} %get-tuple-element.5.own_ref), channel_id=1, source_target_pairs={{0,1},{1,2},{2,3},{3,4},{4,5},{5,6},{6,7},{8,9},{9,10},{10,11},{11... | collective-permute-start | bytes 4718600 | tf_op jit(solution)/shard_map/ppermute | solution.py:251
  395.8 69.7 %collective-permute-start.3 = (f32[4,6,128,128]{3,2,1,0:T(8,128)}, f32[4,6,128,128]{3,2,1,0:T(8,128)}, u32[]{:S(2)}, u32[]{:S(2)}) collective-permute-start(f32[4,6,128,128]{3,2,1,0:T(8,128)} %get-tuple-element.5.own_ref), channel_id=1, source_target_pairs={{1,0},{2,1},{3,2},{4,3},{5,4},{6,5},{7,6},{9,8},{10,9},{11,10},{12... | collective-permute-start | bytes 4718600 | tf_op jit(solution)/shard_map/ppermute | solution.py:252
  409.3 56.3 %copy-start.2 = (f32[4,6,128,128]{3,2,1,0:T(8,128)}, f32[4,6,128,128]{3,2,1,0:T(8,128)S(1)}, u32[]{:S(2)}) copy-start(f32[4,6,128,128]{3,2,1,0:T(8,128)S(1)} %collective-permute-done.refs_0_) | copy-start | bytes 4718596
  414.0 51.6 %copy-start.3 = (f32[4,6,128,128]{3,2,1,0:T(8,128)}, f32[4,6,128,128]{3,2,1,0:T(8,128)S(1)}, u32[]{:S(2)}) copy-start(f32[4,6,128,128]{3,2,1,0:T(8,128)S(1)} %collective-permute-done.1.refs_1_) | copy-start | bytes 4718596
